TPU v7x, 32 devices: a 4x4x1 block of a 4x4x8 slice. The times are simulated.
32 devices in a mesh: rep: 2 (over z, core), dp: 16 (over x, y).
Axes of the slice: x: 4, y: 4, z: 1, core: 2. Of those that a mesh axis runs over, the one named last changes fastest.
The devices are a block of a 4x4x8 slice.
Arguments:
- g_w_gate: bfloat16 [32, 2, 1024, 3328], P(('rep', 'dp')), parts along dimension 0
- g_w_up: bfloat16 [32, 2, 1024, 3328], P(('rep', 'dp')), parts along dimension 0
- g_w_down: bfloat16 [32, 2, 3328, 1024], P(('rep', 'dp')), parts along dimension 0
- w_gate: bfloat16 [2, 1024, 3328], replicated
- w_up: bfloat16 [2, 1024, 3328], replicated
- w_down: bfloat16 [2, 3328, 1024], replicated
- m_w_gate: float32 [2, 1024, 3328], P(None, 'dp')
- m_w_up: float32 [2, 1024, 3328], P(None, 'dp')
- m_w_down: float32 [2, 3328, 1024], P(None, 'dp')
- v_w_gate: float32 [2, 1024, 3328], P(None, 'dp')
- v_w_up: float32 [2, 1024, 3328], P(None, 'dp')
- v_w_down: float32 [2, 3328, 1024], P(None, 'dp')
Outputs:
- output 1: bfloat16 [4, 1024, 3328], P('rep'), parts along dimension 0
- output 2: bfloat16 [4, 1024, 3328], P('rep'), parts along dimension 0
- output 3: bfloat16 [4, 3328, 1024], P('rep'), parts along dimension 0
- output 4: float32 [4, 1024, 3328], P('rep', 'dp'), parts along dimension 0
- output 5: float32 [4, 1024, 3328], P('rep', 'dp'), parts along dimension 0
- output 6: float32 [4, 3328, 1024], P('rep', 'dp'), parts along dimension 0
- output 7: float32 [4, 1024, 3328], P('rep', 'dp'), parts along dimension 0
- output 8: float32 [4, 1024, 3328], P('rep', 'dp'), parts along dimension 0
- output 9: float32 [4, 3328, 1024], P('rep', 'dp'), parts along dimension 0
There are 2 independent parts. A program takes and returns all parts, laid end to end along the dimension named above; an argument that names none is the same for every part.
All inputs are finite; a program needn't handle non-finite values.
Results may differ from a plain program's by a relative error of at most 0.022.
Values are sent between devices in bfloat16 or wider.
A program may use at most 768 MiB of HBM per device.

v0:
```python
import jax
import jax.numpy as jnp
from jax import lax
from jax.sharding import PartitionSpec as P


def adamw(w, m, v, g):
    m = 0.9 * m + 0.1 * g
    v = 0.95 * v + 0.05 * g * g
    step = m * lax.rsqrt(v + 1e-8) + 0.1 * w
    return (w - 0.02 * step).astype(jnp.bfloat16), m, v


def solution(mesh):
    def step(*arrays):
        terms, weights, m, v = (arrays[i : i + 3] for i in (0, 3, 6, 9))
        gradients = [lax.psum_scatter(t[0], "dp", scatter_dimension=1, tiled=True).astype(jnp.float32) for t in terms]
        me = lax.axis_index("dp")
        own = [lax.dynamic_slice_in_dim(w, me * one.shape[1], one.shape[1], 1).astype(jnp.float32) for w, one in zip(weights, m, strict=True)]
        new = [adamw(w, m, v, g) for w, m, v, g in zip(own, m, v, gradients, strict=True)]
        whole = [lax.all_gather(one[0], "dp", axis=1, tiled=True) for one in new]
        return (*whole, *(one[1] for one in new), *(one[2] for one in new))

    all_of, cut = P(None, None, None), P(None, "dp", None)
    return jax.shard_map(
        step,
        mesh=mesh,
        in_specs=(P(("rep", "dp"), None, None, None),) * 3 + (all_of,) * 3 + (cut,) * 6,
        out_specs=(P("rep", None, None),) * 3 + (P("rep", "dp", None),) * 6,
        check_vma=False,
    )
```

profile of v0, /device:TPU:97, one launch (start us, length us, event | category | flops | bytes accessed | tf_op | source)
XLA Modules:
  0.0 604.8 jit_solution(2895283611499452541)
XLA Ops:
  7.2 0.1 reduce-scatter.8.cloned.1.call-start
  7.3 0.7 reduce-scatter.8.cloned.1.call-update
  8.0 0.1 reduce-scatter.6.cloned.1.call-start
  8.1 0.7 reduce-scatter.6.cloned.1.call-update
  8.8 0.1 reduce-scatter.4.cloned.1.call-start
  8.9 0.7 reduce-scatter.4.cloned.1.call-update
  9.6 0.1 all-gather.8.cloned.1.call-start
  9.7 96.8 %reduce-scatter.8.cloned.1.call-done = bf16[2,208,1024]{2,1,0:T(8,128)(2,1)} async-done(((bf16[2,3328,1024]{2,1,0:T(8,128)(2,1)}), bf16[2,208,1024]{2,1,0:T(8,128)(2,1)}) %reduce-scatter.8.cloned.1.call-update) | async-done | bytes 851984 | tf_op jit(solution)/shard_map/reduce_scatter | solution.py:17
  106.5 4.0 fusion.10
  110.4 0.1 all-gather.8.cloned.1.call-update
  110.5 0.1 all-gather.6.cloned.1.call-start
  110.6 90.4 %reduce-scatter.6.cloned.1.call-done = bf16[2,64,3328]{2,1,0:T(8,128)(2,1)} async-done(((bf16[2,1024,3328]{2,1,0:T(8,128)(2,1)}), bf16[2,64,3328]{2,1,0:T(8,128)(2,1)}) %reduce-scatter.6.cloned.1.call-update) | async-done | bytes 851984 | tf_op jit(solution)/shard_map/reduce_scatter | solution.py:17
  200.9 5.1 fusion.6
  206.1 0.1 all-gather.4.cloned.1.call-start
  206.1 89.3 %reduce-scatter.4.cloned.1.call-done = bf16[2,64,3328]{2,1,0:T(8,128)(2,1)} async-done(((bf16[2,1024,3328]{2,1,0:T(8,128)(2,1)}), bf16[2,64,3328]{2,1,0:T(8,128)(2,1)}) %reduce-scatter.4.cloned.1.call-update) | async-done | bytes 851984 | tf_op jit(solution)/shard_map/reduce_scatter | solution.py:17
  295.5 3.9 fusion.2
  299.3 0.1 all-gather.4.cloned.1.call-update
  299.4 87.9 %all-gather.8.cloned.1.call-done = bf16[2,3328,1024]{2,1,0:T(8,128)(2,1)} async-done(((bf16[2,208,1024]{2,1,0:T(8,128)(2,1)}), bf16[2,3328,1024]{2,1,0:T(8,128)(2,1)}) %all-gather.8.cloned.1.call-update) | async-done | bytes 13631504 | tf_op jit(solution)/shard_map/all_gather | solution.py:21
  387.2 91.7 %all-gather.6.cloned.1.call-done = bf16[2,1024,3328]{2,1,0:T(8,128)(2,1)} async-done(((bf16[2,64,3328]{2,1,0:T(8,128)(2,1)}), bf16[2,1024,3328]{2,1,0:T(8,128)(2,1)}) %all-gather.6.cloned.1.call-update) | async-done | bytes 13631504 | tf_op jit(solution)/shard_map/all_gather | solution.py:21
  478.9 91.7 %all-gather.4.cloned.1.call-done = bf16[2,1024,3328]{2,1,0:T(8,128)(2,1)} async-done(((bf16[2,64,3328]{2,1,0:T(8,128)(2,1)}), bf16[2,1024,3328]{2,1,0:T(8,128)(2,1)}) %all-gather.4.cloned.1.call-update) | async-done | bytes 13631504 | tf_op jit(solution)/shard_map/all_gather | solution.py:21
  570.7 15.1 %copy.24 = bf16[2,1024,3328]{2,1,0:T(8,128)(2,1)} copy(bf16[2,1024,3328]{2,1,0:T(8,128)(2,1)} %all-gather.4.cloned.1.call-done) | data formatting | bytes 27262976
  585.7 6.6 %copy.25 = bf16[2,1024,3328]{2,1,0:T(8,128)(2,1)} copy(bf16[2,1024,3328]{2,1,0:T(8,128)(2,1)S(1)} %copy-done) | data formatting | bytes 27262976
  592.3 0.5 slice-done.3
  592.8 5.1 copy.26
  (19 shorter events, 0.1 us)
Async XLA Ops:
  7.2 99.3 %reduce-scatter.8.cloned.1.call-start = ((), (), s32[]{:S(2)}) async-start(), calls=%async_computation.7 | async-start | bytes 14483456 | tf_op jit(solution)/shard_map/reduce_scatter | solution.py:17
  8.0 192.9 %reduce-scatter.6.cloned.1.call-start = ((), (), s32[]{:S(2)}) async-start(), calls=%async_computation.5 | async-start | bytes 14483456 | tf_op jit(solution)/shard_map/reduce_scatter | solution.py:17
  8.8 286.7 %reduce-scatter.4.cloned.1.call-start = ((), (), s32[]{:S(2)}) async-start(), calls=%async_computation.3 | async-start | bytes 14483456 | tf_op jit(solution)/shard_map/reduce_scatter | solution.py:17
  8.9 97.6 %copy-start.1 = (f32[2,208,1024]{2,1,0:T(8,128)S(1)}, f32[2,208,1024]{2,1,0:T(8,128)}, u32[]{:S(2)}) copy-start(f32[2,208,1024]{2,1,0:T(8,128)} %param.23) | copy-start | bytes 5111812
  8.9 97.6 %copy-start.2 = (f32[2,208,1024]{2,1,0:T(8,128)S(1)}, f32[2,208,1024]{2,1,0:T(8,128)}, u32[]{:S(2)}) copy-start(f32[2,208,1024]{2,1,0:T(8,128)} %param.20) | copy-start | bytes 5111812
  9.6 377.6 %all-gather.8.cloned.1.call-start = ((), (), s32[]{:S(2)}) async-start(), calls=%async_computation.8 | async-start | bytes 14483456 | tf_op jit(solution)/shard_map/all_gather | solution.py:21
  110.5 368.5 %all-gather.6.cloned.1.call-start = ((), (), s32[]{:S(2)}) async-start(), calls=%async_computation.6 | async-start | bytes 14483456 | tf_op jit(solution)/shard_map/all_gather | solution.py:21
  200.9 94.5 %copy-start.3 = (f32[2,64,3328]{2,1,0:T(8,128)S(1)}, f32[2,64,3328]{2,1,0:T(8,128)}, u32[]{:S(2)}) copy-start(f32[2,64,3328]{2,1,0:T(8,128)} %param.21) | copy-start | bytes 5111812
  200.9 94.5 %copy-start.4 = (f32[2,64,3328]{2,1,0:T(8,128)S(1)}, f32[2,64,3328]{2,1,0:T(8,128)}, u32[]{:S(2)}) copy-start(f32[2,64,3328]{2,1,0:T(8,128)} %param.18) | copy-start | bytes 5111812
  206.1 364.6 %all-gather.4.cloned.1.call-start = ((), (), s32[]{:S(2)}) async-start(), calls=%async_computation.4 | async-start | bytes 14483456 | tf_op jit(solution)/shard_map/all_gather | solution.py:21
  570.7 15.1 %copy-start = (bf16[2,1024,3328]{2,1,0:T(8,128)(2,1)S(1)}, bf16[2,1024,3328]{2,1,0:T(8,128)(2,1)}, u32[]{:S(2)}) copy-start(bf16[2,1024,3328]{2,1,0:T(8,128)(2,1)} %all-gather.6.cloned.1.call-done) | copy-start | bytes 40894468
  570.7 21.6 %slice-start = ((s8[13631488]{0:T(1024)(128)(4,1)}), s8[4194304]{0:T(1024)(128)(4,1)S(1)}, s32[]{:S(2)}) async-start(s8[13631488]{0:T(1024)(128)(4,1)} %bitcast.6), calls=%async_computation.9 | async-start | bytes 8388608
  570.7 21.6 %slice-start.1 = ((s8[13631488]{0:T(1024)(128)(4,1)}), s8[4194304]{0:T(1024)(128)(4,1)S(1)}, s32[]{:S(2)}) async-start(s8[13631488]{0:T(1024)(128)(4,1)} %bitcast.6), calls=%async_computation.10 | async-start | bytes 8388608
  570.7 21.6 %slice-start.2 = ((s8[13631488]{0:T(1024)(128)(4,1)}), s8[4194304]{0:T(1024)(128)(4,1)S(1)}, s32[]{:S(2)}) async-start(s8[13631488]{0:T(1024)(128)(4,1)} %bitcast.6), calls=%async_computation.11 | async-start | bytes 8388608
  585.7 7.1 %slice-start.3 = ((s8[13631488]{0:T(1024)(128)(4,1)}), s8[1048576]{0:T(1024)(128)(4,1)S(1)}, s32[]{:S(2)}) async-start(s8[13631488]{0:T(1024)(128)(4,1)} %bitcast.6), calls=%async_computation.12 | async-start | bytes 2097152
Sparse Core Ops, SparseCore 0:
  11.3 95.0 reduce-scatter.7
  109.8 91.1 reduce-scatter.5
  204.2 91.1 reduce-scatter.3
  297.8 89.3 all-gather.7
  389.6 89.2 all-gather.5
  481.3 89.2 all-gather.3
where the time goes:
time: 605 us
  waiting for transfers between devices  550 us (91%)
  local copies, waits for them, and re-layouts  27.3 us (5%)
  between operations  14.2 us (2%)
  other arithmetic  12.9 us (2%)
    reduce_scatter x3, waiting for transfers between devices, step(): lax.psum_scatter(t[0], 'dp', scatter_dimension=1, tiled=True)  276 us
    all_gather x3, waiting for transfers between devices, step(): whole = [lax.all_gather(one[0], 'dp', axis=1, tiled=True) for one in new]  271 us
    unnamed x21, local copies, waits for them, and re-layouts  27.3 us
    convert_element_type x3, other arithmetic, adamw(): return ((w - 0.02 * step).astype(jnp.bfloat16), m, v)  12.9 us
  transfers between devices with their start and end apart: 6, of which 6 were waited for; matrix products, arithmetic and copies ran while one was open for 2% of the time, Pallas kernels for 0%

commit v1 on v0

v1 whole, which is shorter than its diff:
```python
import math

import jax
import jax.numpy as jnp
from jax import lax
from jax.experimental import pallas as pl
from jax.experimental.pallas import tpu as pltpu
from jax.sharding import PartitionSpec as P

MESH = pl.DeviceIdType.MESH
ROWS, COLS = 16, 256
MESSAGES = 36


def adamw(w, m, v, g):
    m = 0.9 * m + 0.1 * g
    v = 0.95 * v + 0.05 * g * g
    step = m * lax.rsqrt(v + 1e-8) + 0.1 * w
    return (w - 0.02 * step).astype(jnp.bfloat16), m, v


def kernel(side, *refs):
    terms, weights, ms, vs, outs, gs = (refs[i : i + 3] for i in range(0, 18, 3))
    own, first, second = (refs[i : i + 3] for i in (18, 21, 24))
    wide, narrow = refs[27:30], refs[30:33]
    send_sem, recv_sem, load_sem, moment_sem, store_sem = (refs[i : i + 3] for i in range(33, 48, 3))

    me = lax.axis_index("dp")
    x, y = me // side, me % side
    for neighbour in ((x + 1) % side * side + y, (x + side - 1) % side * side + y, x * side + (y + 1) % side, x * side + (y + side - 1) % side):
        pl.semaphore_signal(pltpu.get_barrier_semaphore(), inc=1, device_id={"dp": neighbour}, device_id_type=MESH)
    pl.semaphore_wait(pltpu.get_barrier_semaphore(), 4)

    def place(layer):
        return x * (1 - layer) + y * layer, x * layer + y * (1 - layer)

    def index(layer, p, q):
        return (p + 2 * side) % side * (side * (1 - layer) + layer) + (q + 2 * side) % side * (1 - layer + side * layer)

    def to(layer, ring, by):
        p, q = place(layer)
        return {"dp": index(layer, p + by, q) if ring == 0 else index(layer, p, q + by)}

    def part(w, half):
        size = own[w].shape[2]
        cut = (size // ROWS + 1) // 2 * ROWS
        return (pl.ds(0, cut), pl.ds(cut, size - cut), pl.ds(0, size))[half]

    def half_of(k):
        return 2 if k < 12 or k >= 24 else (0, 1, 1, 0, 0, 1, 0, 1, 0, 1, 0, 1)[k - 12]

    def rows(w, layer, p, q, half=2):
        size = own[w].shape[2]
        inside = part(w, half)
        return pl.ds(pl.multiple_of(index(layer, p, q) * size + inside.start, ROWS), inside.size)

    def send(w, layer, k, source, target, device):
        pltpu.make_async_remote_copy(source, target, send_sem[w].at[layer, k], recv_sem[w].at[layer, k], device_id=device, device_id_type=MESH).start()

    def wait(w, layer, k, half=2):
        shape = own[w].at[layer, 0, part(w, half)]
        pltpu.make_async_copy(shape, shape, recv_sem[w].at[layer, k]).wait()

    def over_layers(f, times=1):
        def body(n, _):
            f(n % 2, n // 2) if times > 1 else f(n)
            return 0

        lax.fori_loop(0, 2 * times, body, 0)

    def blockwise(w, half, f):
        inside = part(w, half)

        def body(r, _):
            at = pl.ds(pl.multiple_of(inside.start + r * ROWS, ROWS), ROWS)
            for c in range(0, own[w].shape[3], COLS):
                f(at, pl.ds(c, COLS))
            return 0

        lax.fori_loop(0, inside.size // ROWS, body, 0)

    def add(w, layer, half, slot, *others):
        def one(at, c):
            total = own[w][layer, slot, at, c].astype(jnp.float32)
            for ref, other in others:
                total += ref[layer, other, at, c].astype(jnp.float32)
            own[w][layer, slot, at, c] = total.astype(jnp.bfloat16)

        blockwise(w, half, one)

    def load(w, layer, slot):
        p, q = place(layer)
        if isinstance(slot, int) and slot >= 4:
            at = rows(w, layer, p, q + slot - 4)
        else:
            at = rows(w, layer, p + (1 if slot < 2 else -1), q + (2, 1, 3, 0)[slot])
        return pltpu.make_async_copy(terms[w].at[0, layer, at], own[w].at[layer, slot], load_sem[w].at[layer, slot])


    def loads(w):
        def f(layer):
            for slot in range(8):
                load(w, layer, slot).start()

        over_layers(f)

    def raw1(w):
        def g(layer, j):
            p, q = place(layer)
            i = j % 2
            for k, d, by in ((0, 2 - i, 1), (2, 3 - 3 * i, -1)):
                source = terms[w].at[0, layer, rows(w, layer, p + 2, q + d)]
                send(w, layer, k + i, source, first[w].at[layer, k + i], to(layer, 0, by))

        def h(layer, i):
            p, q = place(layer)
            for k, d, by in ((4, 3 - 3 * i, 1), (6, 2 - i, -1)):
                source = terms[w].at[0, layer, rows(w, layer, p + by, q + d)]
                send(w, layer, k + i, source, first[w].at[layer, k + i], to(layer, 0, by))

        over_layers(g, 2)
        over_layers(h, 2)

    def fwd1(w):
        for i in range(2):

            def f(layer, i=i):
                for k, slot, by in ((0, 0, 1), (2, 2, -1)):
                    load(w, layer, slot + i).wait()
                    wait(w, layer, k + i)
                    add(w, layer, 2, slot + i, (first[w], k + i))
                    send(w, layer, 8 + k + i, own[w].at[layer, slot + i], first[w].at[layer, 8 + k + i], to(layer, 0, by))

            over_layers(f)

    def raw2(w):
        def f(layer):
            load(w, layer, 6).wait()
            wait(w, layer, 8)
            wait(w, layer, 6)
            add(w, layer, 2, 6, (first[w], 8), (first[w], 6))
            for half, by in ((0, 1), (1, -1)):
                at = part(w, half)
                send(w, layer, 12 + half, own[w].at[layer, 6, at], second[w].at[layer, 0, at], to(layer, 1, by))

        def g(layer):
            load(w, layer, 5).wait()
            wait(w, layer, 9)
            wait(w, layer, 7)
            add(w, layer, 1, 5, (first[w], 9), (first[w], 7))
            at = part(w, 1)
            send(w, layer, 14, own[w].at[layer, 5, at], second[w].at[layer, 1, at], to(layer, 1, 1))
            load(w, layer, 7).wait()
            wait(w, layer, 4)
            wait(w, layer, 10)
            add(w, layer, 0, 7, (first[w], 4), (first[w], 10))
            at = part(w, 0)
            send(w, layer, 15, own[w].at[layer, 7, at], second[w].at[layer, 2, at], to(layer, 1, -1))

        over_layers(f)
        over_layers(g)

    def fwd2(w):
        def f(layer):
            wait(w, layer, 12, 0)
            add(w, layer, 0, 5, (first[w], 9), (first[w], 7), (second[w], 0))
            at = part(w, 0)
            send(w, layer, 16, own[w].at[layer, 5, at], second[w].at[layer, 1, at], to(layer, 1, 1))
            wait(w, layer, 13, 1)
            add(w, layer, 1, 7, (first[w], 4), (first[w], 10), (second[w], 0))
            at = part(w, 1)
            send(w, layer, 17, own[w].at[layer, 7, at], second[w].at[layer, 2, at], to(layer, 1, -1))

        over_layers(f)

    def moments(w, layer):
        p, q = place(layer)
        slot = layer if w < 2 else 0
        return (
            pltpu.make_async_copy(ms[w].at[layer], wide[w].at[slot, 0], moment_sem[w].at[layer, 0]),
            pltpu.make_async_copy(vs[w].at[layer], wide[w].at[slot, 1], moment_sem[w].at[layer, 1]),
            pltpu.make_async_copy(weights[w].at[layer, rows(w, layer, p, q)], narrow[w].at[slot], moment_sem[w].at[layer, 2]),
        )

    def load_moments(w):
        def f(layer):
            for copy in moments(w, layer):
                copy.start()

        over_layers(f)

    def store(w, layer):
        p, q = place(layer)
        return (
            pltpu.make_async_copy(own[w].at[layer, 4], gs[w].at[layer], store_sem[w].at[layer, 0]),
            pltpu.make_async_copy(second[w].at[layer, 1], outs[w].at[layer, rows(w, layer, p, q)], store_sem[w].at[layer, 1]),
        )

    def step(w):
        def f(layer):
            p, q = place(layer)
            slot = layer if w < 2 else 0
            if w == 2:
                for copy in moments(w, layer):
                    copy.start()
            load(w, layer, 4).wait()
            for k, half in ((5, 2), (11, 2), (14, 1), (15, 0), (16, 0), (17, 1)):
                wait(w, layer, k, half)
            for copy in moments(w, layer):
                copy.wait()

            def one(at, c):
                total = own[w][layer, 4, at, c].astype(jnp.float32)
                for ref, other in ((first[w], 5), (first[w], 11), (second[w], 1), (second[w], 2)):
                    total += ref[layer, other, at, c].astype(jnp.float32)
                g = total.astype(jnp.bfloat16)
                own[w][layer, 4, at, c] = g
                old = narrow[w][slot, at, c].astype(jnp.float32)
                second[w][layer, 1, at, c] = adamw(old, wide[w][slot, 0, at, c], wide[w][slot, 1, at, c], g.astype(jnp.float32))[0]

            blockwise(w, 2, one)
            for k, half, by in ((18, 0, 1), (21, 1, -1), (19, 1, 1), (20, 0, -1)):
                source = second[w].at[layer, 1, part(w, half)]
                send(w, layer, k, source, outs[w].at[layer, rows(w, layer, p, q, half)], to(layer, 1, by))
            for copy in store(w, layer):
                copy.start()

        over_layers(f)

    def gather2(w):
        def f(layer):
            p, q = place(layer)
            for k, half, by in ((18, 0, 1), (21, 1, -1)):
                wait(w, layer, k, half)
                at = rows(w, layer, p, q - by, half)
                send(w, layer, 22 + half, outs[w].at[layer, at], outs[w].at[layer, at], to(layer, 1, by))

        over_layers(f)

    def both_ways(w, layer, d, source):
        p, q = place(layer)
        at = rows(w, layer, p, q + d)
        for k, by in ((24, 1), (28, -1)):
            send(w, layer, k + d, outs[w].at[layer, at] if source is None else source, outs[w].at[layer, at], to(layer, 0, by))

    def gather1(w):
        def f(layer):
            both_ways(w, layer, 0, second[w].at[layer, 1])
            wait(w, layer, 20, 0)
            both_ways(w, layer, 1, None)
            wait(w, layer, 19, 1)
            both_ways(w, layer, 3, None)

        over_layers(f)

    def gather1_far(w):
        def f(layer):
            wait(w, layer, 22, 0)
            wait(w, layer, 23, 1)
            both_ways(w, layer, 2, None)

        over_layers(f)

    def gather1_on(w):
        def f(layer, i):
            p, q = place(layer)
            for k, d, by in ((24, 2 * i, 1), (28, 1 + 2 * i, -1)):
                wait(w, layer, k + d)
                at = rows(w, layer, p - by, q + d)
                send(w, layer, (32 if by == 1 else 34) + i, outs[w].at[layer, at], outs[w].at[layer, at], to(layer, 0, by))

        over_layers(f, 2)

    def finish(w):
        def f(layer):
            for k in (25, 27, 28, 30, 32, 33, 34, 35):
                wait(w, layer, k)
            for k in range(MESSAGES):
                shape = own[w].at[layer, 0, part(w, half_of(k))]
                pltpu.make_async_copy(shape, shape, send_sem[w].at[layer, k]).wait()
            for copy in store(w, layer):
                copy.wait()

        over_layers(f)

    raw1(0)
    loads(0)
    load_moments(0)
    loads(1)
    fwd1(0)
    raw1(1)
    loads(2)
    raw2(0)
    fwd1(1)
    raw1(2)
    fwd2(0)
    raw2(1)
    fwd1(2)
    step(0)
    load_moments(1)
    fwd2(1)
    raw2(2)
    gather2(0)
    gather1(0)
    step(1)
    fwd2(2)
    gather1_far(0)
    gather2(1)
    gather1(1)
    step(2)
    gather1_on(0)
    gather1_far(1)
    gather2(2)
    gather1(2)
    gather1_on(1)
    gather1_far(2)
    gather1_on(2)
    for w in range(3):
        finish(w)


def solution(mesh):
    n = mesh.shape["dp"]
    side = math.isqrt(n)

    def step(*arrays):
        terms, weights, m, v = (arrays[i : i + 3] for i in (0, 3, 6, 9))
        blocks = [(one.shape[1], one.shape[2]) for one in m]
        layers = m[0].shape[0]
        anywhere = pl.BlockSpec(memory_space=pl.ANY)
        scratch = []
        for count in (8, 12, 3):
            scratch += [pltpu.VMEM((layers, count, *b), jnp.bfloat16) for b in blocks]
        kept = [2, 2, 1]
        wide = [pltpu.VMEM((k, 2, *b), jnp.float32) for k, b in zip(kept, blocks)]
        narrow = [pltpu.VMEM((k, *b), jnp.bfloat16) for k, b in zip(kept, blocks)]
        wide, narrow = [wide[0], wide[2]], [narrow[0], narrow[2]]
        for count in (MESSAGES, MESSAGES, 8, 3, 2):
            scratch += [pltpu.SemaphoreType.DMA((layers, count))] * 3

        def body(*refs):
            head, buffers, rest = refs[:27], refs[27:31], refs[31:]
            wide = (buffers[0], buffers[0], buffers[1])
            narrow = (buffers[2], buffers[2], buffers[3])
            kernel(side, *head, *wide, *narrow, *rest)

        scratch = scratch[:9] + wide + narrow + scratch[9:]
        result = pl.pallas_call(
            body,
            out_shape=[jax.ShapeDtypeStruct(w.shape, w.dtype) for w in weights] + [jax.ShapeDtypeStruct(one.shape, jnp.bfloat16) for one in m],
            in_specs=[anywhere] * 12,
            out_specs=[anywhere] * 6,
            scratch_shapes=scratch,
            compiler_params=pltpu.CompilerParams(collective_id=0, has_side_effects=True, vmem_limit_bytes=67043328),
            name="step",
        )(*arrays)
        whole, g = result[:3], result[3:]
        new = [adamw(0.0, one, two, three.astype(jnp.float32)) for one, two, three in zip(m, v, g)]
        return (*whole, *(one[1] for one in new), *(one[2] for one in new))

    all_of, cut = P(None, None, None), P(None, "dp", None)
    return jax.shard_map(
        step,
        mesh=mesh,
        in_specs=(P(("rep", "dp"), None, None, None),) * 3 + (all_of,) * 3 + (cut,) * 6,
        out_specs=(P("rep", None, None),) * 3 + (P("rep", "dp", None),) * 6,
        check_vma=False,
    )
```

time: 605 us -> 461 us (0.76)
  waiting for transfers between devices: 550 us -> 0 us
  Pallas kernels: 0 us -> 425 us
  between operations: 14.2 us -> 0.71 us
    pallas_call x0 -> x1, Pallas kernels: none -> 425 us  [step(): pl.pallas_call(body, out_shape=[jax.ShapeDtypeStruct(w.shape, w.dtype) fo...]
    reduce_scatter x3 -> x0, waiting for transfers between devices: 276 us -> none  [step(): lax.psum_scatter(t[0], 'dp', scatter_dimension=1, tiled=True)]
    all_gather x3 -> x0, waiting for transfers between devices: 271 us -> none  [step(): whole = [lax.all_gather(one[0], 'dp', axis=1, tiled=True) for one in new]]
    add x0 -> x2, other arithmetic: none -> 12.9 us  [adamw(): v = 0.95 * v + 0.05 * g * g]
    convert_element_type x3 -> x0, other arithmetic: 12.9 us -> none  [adamw(): return ((w - 0.02 * step).astype(jnp.bfloat16), m, v)]
  transfers between devices with their start and end apart: 6 -> 0, of which waited for: 6 -> 0; matrix products, arithmetic and copies ran while one was open for 2% -> 0% of each run, Pallas kernels for 0% -> 0%
where the time goes in v1:
time: 461 us
  Pallas kernels  425 us (92%)
  local copies, waits for them, and re-layouts  22.4 us (5%)
  other arithmetic  12.9 us (3%)
    pallas_call x1, Pallas kernels, step(): pl.pallas_call(body, out_shape=[jax.ShapeDtypeStruct(w.shape, w.dtype) fo...  425 us
    unnamed x21, local copies, waits for them, and re-layouts  22.4 us
    add x2, other arithmetic, adamw(): v = 0.95 * v + 0.05 * g * g  12.9 us

profile of v1, /device:TPU:97, one launch (start us, length us, event | category | flops | bytes accessed | tf_op | source)
XLA Modules:
  0.0 460.7 jit_solution(332305995031744480)
XLA Ops:
  0.6 424.7 %step.1 = (bf16[2,1024,3328]{2,1,0:T(8,128)(2,1)}, bf16[2,1024,3328]{2,1,0:T(8,128)(2,1)}, bf16[2,3328,1024]{2,1,0:T(8,128)(2,1)}, bf16[2,64,3328]{2,1,0:T(8,128...) custom-call(bf16[1,2,1024,3328]{3,2,1,0:T(8,128)(2,1)} %refs_0_.1, ...), custom_call_target="tpu_custom_call" | custom-call | tf_op jit(solution)/shard_map/step/pallas_call | solution.py:348
  425.3 0.0 copy-start
  425.3 0.0 slice-start.4
  425.3 0.0 slice-start.5
  425.3 7.3 %fusion.3 = (f32[2,64,3328]{2,1,0:T(8,128)}, f32[2,64,3328]{2,1,0:T(8,128)}, f32[2,64,3328]{2,1,0:T(8,128)}, f32[2,64,3328]{2,1,0:T(8,128)}) fusion(bf16[2,64,3328]{2,1,0:T(8,128)(2,1)} %get-tuple-element.18, f32[2,64,3328]{2,1,0:T(8,128)} %refs_9_.1, f32[2,64,3328]{2,1,0:T(8,128)} %refs_6_.1, bf16[2,64,3328]{2,1,0:T(8,128)(2,1)} %get-tuple-element.19, ...), kind=kLoop, calls=%fused_computation.9 | loop fusion | flops 6815744 | bytes 15335424 | tf_op jit(solution)/shard_map/add | solution.py:17
  432.7 5.6 %fusion.5 = (f32[2,208,1024]{2,1,0:T(8,128)}, f32[2,208,1024]{2,1,0:T(8,128)}) fusion(bf16[2,208,1024]{2,1,0:T(8,128)(2,1)} %get-tuple-element.20, f32[2,208,1024]{2,1,0:T(8,128)} %refs_11_.1, f32[2,208,1024]{2,1,0:T(8,128)} %refs_8_.1), kind=kLoop, calls=%fused_computation.11 | loop fusion | flops 3407872 | bytes 7667712 | tf_op jit(solution)/shard_map/add | solution.py:17
  438.3 0.0 copy-done
  438.3 0.0 slice-start.6
  438.3 0.0 slice-start.7
  438.3 0.0 slice-start
  438.3 0.0 slice-start.1
  438.3 6.9 %copy.24 = bf16[2,1024,3328]{2,1,0:T(8,128)(2,1)} copy(bf16[2,1024,3328]{2,1,0:T(8,128)(2,1)S(1)} %copy-done) | data formatting | bytes 27262976
  445.2 0.0 slice-done.4
  445.2 0.0 slice-done.5
  445.2 0.0 slice-done.6
  445.2 1.5 slice-done.7
  446.7 0.0 slice-start.2
  446.7 0.0 slice-start.3
  446.7 6.9 %copy.25 = bf16[2,1024,3328]{2,1,0:T(8,128)(2,1)} copy(bf16[2,1024,3328]{2,1,0:T(8,128)(2,1)S(1)} %bitcast.3) | data formatting | bytes 27262976
  453.6 0.0 slice-done
  453.6 0.0 slice-done.1
  453.6 1.7 slice-done.2
  455.3 0.2 slice-done.3
  455.6 5.1 %copy.26 = bf16[2,3328,1024]{2,1,0:T(8,128)(2,1)} copy(bf16[2,3328,1024]{2,1,0:T(8,128)(2,1)S(1)} %bitcast.1) | data formatting | bytes 27262976
  (2 shorter events, 0.0 us)
Async XLA Ops:
  425.3 13.0 %copy-start = (bf16[2,1024,3328]{2,1,0:T(8,128)(2,1)S(1)}, bf16[2,1024,3328]{2,1,0:T(8,128)(2,1)}, u32[]{:S(2)}) copy-start(bf16[2,1024,3328]{2,1,0:T(8,128)(2,1)} %get-tuple-element.38) | copy-start | bytes 40894468
  425.3 19.9 %slice-start.4 = ((s8[13631488]{0:T(1024)(128)(4,1)}), s8[1048576]{0:T(1024)(128)(4,1)S(1)}, s32[]{:S(2)}) async-start(s8[13631488]{0:T(1024)(128)(4,1)} %bitcast.2), calls=%async_computation.4 | async-start | bytes 2097152
  425.3 19.9 %slice-start.5 = ((s8[13631488]{0:T(1024)(128)(4,1)}), s8[4194304]{0:T(1024)(128)(4,1)S(1)}, s32[]{:S(2)}) async-start(s8[13631488]{0:T(1024)(128)(4,1)} %bitcast.2), calls=%async_computation.5 | async-start | bytes 8388608
  438.3 6.9 %slice-start.6 = ((s8[13631488]{0:T(1024)(128)(4,1)}), s8[4194304]{0:T(1024)(128)(4,1)S(1)}, s32[]{:S(2)}) async-start(s8[13631488]{0:T(1024)(128)(4,1)} %bitcast.2), calls=%async_computation.6 | async-start | bytes 8388608
  438.3 8.4 %slice-start.7 = ((s8[13631488]{0:T(1024)(128)(4,1)}), s8[4194304]{0:T(1024)(128)(4,1)S(1)}, s32[]{:S(2)}) async-start(s8[13631488]{0:T(1024)(128)(4,1)} %bitcast.2), calls=%async_computation.7 | async-start | bytes 8388608
  438.3 15.3 %slice-start = ((s8[13631488]{0:T(1024)(128)(4,1)}), s8[4194304]{0:T(1024)(128)(4,1)S(1)}, s32[]{:S(2)}) async-start(s8[13631488]{0:T(1024)(128)(4,1)} %bitcast), calls=%async_computation | async-start | bytes 8388608
  438.3 15.3 %slice-start.1 = ((s8[13631488]{0:T(1024)(128)(4,1)}), s8[4194304]{0:T(1024)(128)(4,1)S(1)}, s32[]{:S(2)}) async-start(s8[13631488]{0:T(1024)(128)(4,1)} %bitcast), calls=%async_computation.1 | async-start | bytes 8388608
  446.7 8.7 %slice-start.2 = ((s8[13631488]{0:T(1024)(128)(4,1)}), s8[4194304]{0:T(1024)(128)(4,1)S(1)}, s32[]{:S(2)}) async-start(s8[13631488]{0:T(1024)(128)(4,1)} %bitcast), calls=%async_computation.2 | async-start | bytes 8388608
  446.7 8.9 %slice-start.3 = ((s8[13631488]{0:T(1024)(128)(4,1)}), s8[1048576]{0:T(1024)(128)(4,1)S(1)}, s32[]{:S(2)}) async-start(s8[13631488]{0:T(1024)(128)(4,1)} %bitcast), calls=%async_computation.3 | async-start | bytes 2097152
